TPU v7x, 32 devices: a whole 2x2x4 slice. The times are simulated.
32 devices in a mesh: node: 2 (over y), space: 16 (over z, x, core).
Axes of the slice: x: 2, y: 2, z: 4, core: 2. Of those that a mesh axis runs over, the one named last changes fastest.
Arguments:
- u_start: float32 [128, 256, 128], P('space'), may hold values from 0 to 1
- v_start: float32 [128, 256, 128], P('space'), may hold values from 0 to 2
- labels: int32 [128, 256, 128], P('space'), may hold values from 0 to 2
- u_guess: float32 [4, 128, 256, 128], P('node', 'space'), may hold values from 0 to 1
- v_guess: float32 [4, 128, 256, 128], P('node', 'space'), may hold values from 0 to 2
Outputs:
- u_nodes: float32 [4, 128, 256, 128], P('node', 'space')
- v_nodes: float32 [4, 128, 256, 128], P('node', 'space')
Inputs may be any that keep to these rules, and one draw needn't show every extreme that they name: `labels`: 0 marks healthy, 1 fibrous and 2 scar tissue.
All inputs are finite; a program needn't handle non-finite values.
Results may differ from a plain program's by a relative error of at most 0.0001.
Values sent between devices are 32-bit elements; how exact they have to be, the bound alone decides.
A program may use at most 192 MiB of HBM per device.

v0:
```python
import jax
import jax.numpy as jnp
from jax import lax
from jax.sharding import PartitionSpec as P

SWEEPS = 2


radau_points = (0.08858795951270396, 0.4094668644407347, 0.7876594617608471, 1.0)
time_step = 0.16
onset_level = 0.15
ionic_gain = 8.0
recovery_base = 0.002
recovery_slope = 0.2
recovery_offset = 0.3
conductances = (1.0, 0.35, 0.05)
excitability = (1.0, 0.6, 0.0)


def with_halo(block, sides, width):
    for axis, dim in sides:
        count = lax.axis_size(axis)
        forward = [(i, i + 1) for i in range(count - 1)]
        backward = [(target, source) for source, target in forward]
        low = lax.ppermute(
            lax.slice_in_dim(block, block.shape[dim] - width, None, axis=dim), axis, forward
        )
        high = lax.ppermute(lax.slice_in_dim(block, 0, width, axis=dim), axis, backward)
        block = jnp.concatenate([low, block, high], axis=dim)
    return block


def weight_table():
    table = []
    for target in range(4):
        entries = []
        for column in range(4):
            coeffs = [1.0]
            for other in range(4):
                if other != column:
                    factor = 1.0 / (radau_points[column] - radau_points[other])
                    raised = [0.0] + coeffs
                    lowered = coeffs + [0.0]
                    coeffs = [
                        factor * (raised[place] - radau_points[other] * lowered[place])
                        for place in range(len(raised))
                    ]
            integral = 0.0
            for place in range(len(coeffs)):
                integral = integral + coeffs[place] * radau_points[target] ** (place + 1) / (
                    place + 1
                )
            entries.append(time_step * integral)
        table.append(entries)
    return table


def label_values(labels, values):
    return jnp.where(
        labels == 0,
        jnp.float32(values[0]),
        jnp.where(labels == 1, jnp.float32(values[1]), jnp.float32(values[2])),
    )


def face_terms(conduct_ext):
    padded = jnp.pad(conduct_ext, ((0, 0), (1, 1), (1, 1)))
    center = padded[1:-1, 1:-1, 1:-1]
    sides = (
        padded[2:, 1:-1, 1:-1],
        padded[:-2, 1:-1, 1:-1],
        padded[1:-1, 2:, 1:-1],
        padded[1:-1, :-2, 1:-1],
        padded[1:-1, 1:-1, 2:],
        padded[1:-1, 1:-1, :-2],
    )
    result = []
    for beside in sides:
        total = center + beside
        result.append(
            jnp.where(total > 0, 2.0 * center * beside / jnp.where(total > 0, total, 1.0), 0.0)
        )
    return result


def rates(u_ext, v_field, facing, excite):
    padded = jnp.pad(u_ext, ((0, 0), (0, 0), (1, 1), (1, 1)))
    u_field = padded[:, 1:-1, 1:-1, 1:-1]
    sides = (
        padded[:, 2:, 1:-1, 1:-1],
        padded[:, :-2, 1:-1, 1:-1],
        padded[:, 1:-1, 2:, 1:-1],
        padded[:, 1:-1, :-2, 1:-1],
        padded[:, 1:-1, 1:-1, 2:],
        padded[:, 1:-1, 1:-1, :-2],
    )
    spread = jnp.zeros_like(u_field)
    for face_value, voltage_side in zip(facing, sides):
        spread = spread + face_value[None] * (voltage_side - u_field)
    ionic = ionic_gain * u_field * (u_field - onset_level) * (1.0 - u_field) - u_field * v_field
    rate_u = spread + excite[None] * ionic
    recovery = recovery_base + recovery_slope * v_field / jnp.maximum(
        u_field + recovery_offset, recovery_offset
    )
    rate_v = recovery * (-v_field - ionic_gain * u_field * (u_field - onset_level - 1.0))
    return (rate_u, rate_v)


def on_device(u_start, v_start, labels, u_guess, v_guess):
    local_nodes = u_guess.shape[0]
    first_node = lax.axis_index("node") * local_nodes
    weights_all = jnp.asarray(weight_table(), jnp.float32)
    conduct = label_values(labels, conductances)
    excite = label_values(labels, excitability)
    reach = 1
    tissue = with_halo(jnp.stack([conduct, excite]), (("space", 1),), reach)
    u_nodes, v_nodes = (
        lax.all_gather(u_guess, "node", axis=0, tiled=True),
        lax.all_gather(v_guess, "node", axis=0, tiled=True),
    )
    facing = face_terms(tissue[0])
    excite_mid = tissue[1, 1:-1]
    u_now, v_now = (u_nodes, v_nodes)
    for sweep_index in range(SWEEPS):
        bordered = with_halo(u_now, (("space", 1),), 1)
        rate_u, rate_v = rates(bordered, v_now, facing, excite_mid)
        summed_u = jnp.einsum("ij,jabc->iabc", weights_all, rate_u, precision=lax.Precision.HIGHEST)
        summed_v = jnp.einsum("ij,jabc->iabc", weights_all, rate_v, precision=lax.Precision.HIGHEST)
        u_now = u_start[None] + summed_u
        v_now = v_start[None] + summed_v
    u_now = lax.dynamic_slice_in_dim(u_now, first_node, local_nodes, 0)
    v_now = lax.dynamic_slice_in_dim(v_now, first_node, local_nodes, 0)
    return (u_now, v_now)


def solution(mesh):
    return jax.shard_map(
        on_device,
        mesh=mesh,
        in_specs=(
            P("space", None, None),
            P("space", None, None),
            P("space", None, None),
            P("node", "space", None, None),
            P("node", "space", None, None),
        ),
        out_specs=(P("node", "space", None, None), P("node", "space", None, None)),
        check_vma=False,
    )
```

profile of v0, /device:TPU:0, one launch (start us, length us, event | category | flops | bytes accessed | tf_op | source)
XLA Modules:
  0.0 221.8 jit_solution(9188739072148583989)
XLA Ops:
  7.2 0.0 all-gather.3.cloned.1.call-start
  7.2 0.7 all-gather.3.cloned.1.call-update
  7.9 0.0 all-gather.5.cloned.1.call-start
  8.0 0.7 all-gather.5.cloned.1.call-update
  8.7 0.3 fusion.58
  9.0 0.0 copy-start.11
  9.0 0.2 fusion.59
  9.3 1.3 collective-permute-start
  10.6 3.0 %collective-permute-start.2 = (f32[2,1,256,128]{3,2,1,0:T(8,128)S(1)}, f32[2,1,256,128]{3,2,1,0:T(8,128)S(1)}, u32[]{:S(2)}, u32[]{:S(2)}) collective-permute-start(f32[2,1,256,128]{3,2,1,0:T(8,128)S(1)} %get-tuple-element.19), channel_id=1, source_target_pairs={{0,1},{1,2},{2,3},{3,4},{4,5},{5,6},{6,7},{7,8},{8,9},{9,10},{10,1... | collective-permute-start | bytes 786440 | tf_op jit(solution)/shard_map/ppermute | solution.py:25
  13.6 0.0 collective-permute-done
  13.7 1.1 collective-permute-done.2
  14.8 0.7 copy-done.19
  15.5 0.1 fusion.48
  15.6 3.5 %compare_select_fusion.6 = (f32[8,256,128]{2,1,0:T(8,128)S(1)}, f32[8,256,128]{2,1,0:T(8,128)}, f32[8,256,128]{2,1,0:T(8,128)}, f32[8,256,128]{2,1,0:T(8,128)}, f32[8,256,128]{2,1,0:T(8,128)}) fusion(f32[10,256,128]{2,1,0:T(8,128)S(1)} %fusion.48, pred[8,256,128]{2,1,0:T(8,128)(4,1)S(1)} %get-tuple-element.10, pred[8,256,128]{2,1,0:T(8,128)(4,1)S(1)} %get-tuple-element.9), kind=kLoop, calls=%fused_computation.86 | loop fusion | flops 7602176 | bytes 7077888 | tf_op jit(solution)/shard_map/jit(_where)/select_n | solution.py:81
  19.1 49.9 %all-gather.3.cloned.1.call-done = f32[4,8,256,128]{3,2,1,0:T(8,128)} async-done(((f32[2,8,256,128]{3,2,1,0:T(8,128)}), f32[4,8,256,128]{3,2,1,0:T(8,128)}) %all-gather.3.cloned.1.call-update) | async-done | bytes 4194320 | tf_op jit(solution)/shard_map/all_gather | solution.py:118
  69.0 1.4 fusion.62
  70.4 1.4 collective-permute-start.1
  71.9 3.1 %collective-permute-start.3 = (f32[4,1,256,128]{3,2,1,0:T(8,128)S(1)}, f32[4,1,256,128]{3,2,1,0:T(8,128)S(1)}, u32[]{:S(2)}, u32[]{:S(2)}) collective-permute-start(f32[4,1,256,128]{3,2,1,0:T(8,128)S(1)} %get-tuple-element.15), channel_id=1, source_target_pairs={{0,1},{1,2},{2,3},{3,4},{4,5},{5,6},{6,7},{7,8},{8,9},{9,10},{10,1... | collective-permute-start | bytes 1572872 | tf_op jit(solution)/shard_map/ppermute | solution.py:25
  74.9 3.0 %fusion.50 = (f32[8,256,128]{2,1,0:T(8,128)}, f32[8,256,128]{2,1,0:T(8,128)}) fusion(f32[1,8,256,128]{3,2,1,0:T(8,128)S(1)} %get-tuple-element.8, f32[2,1,256,128]{3,2,1,0:T(8,128)} %copy-done.18, f32[1,8,256,128]{3,2,1,0:T(8,128)S(1)} %fusion.59, pred[8,256,128]{2,1,0:T(8,128)(4,1)} %copy-done.11, pred[8,256,128]{2,1,0:T(8,128)(4,1)S(1)} %get-tuple-element.9, ...), kind=kLoop, calls=%fused_computation.97 | loop fusion | flops 4980736 | bytes 5242880 | tf_op jit(solution)/shard_map/mul | solution.py:99
  77.9 0.0 collective-permute-done.1
  78.0 0.0 collective-permute-done.3
  78.0 0.8 copy-done.15
  78.8 0.9 copy-done.16
  79.7 6.5 %select_maximum_fusion.2 = f32[4,10,258,130]{3,2,1,0:T(8,128)} fusion(f32[4,1,256,128]{3,2,1,0:T(8,128)S(1)} %collective-permute-done.1, f32[4,8,256,128]{3,2,1,0:T(8,128)S(1)} %copy-done.4, f32[4,1,256,128]{3,2,1,0:T(8,128)S(1)} %collective-permute-done.3), kind=kLoop, calls=%fused_computation.6 | loop fusion | flops 20124000 | bytes 10609280 | tf_op jit(solution)/shard_map/concatenate | solution.py:29
  86.2 41.1 %all-gather.5.cloned.1.call-done = f32[4,8,256,128]{3,2,1,0:T(8,128)} async-done(((f32[2,8,256,128]{3,2,1,0:T(8,128)}), f32[4,8,256,128]{3,2,1,0:T(8,128)}) %all-gather.5.cloned.1.call-update) | async-done | bytes 4194320 | tf_op jit(solution)/shard_map/all_gather | solution.py:119
  127.3 0.0 copy-done.8
  127.3 19.7 %fusion.19 = (f32[4,8,256,128]{3,2,1,0:T(8,128)S(1)}, f32[4,8,256,128]{3,2,1,0:T(8,128)S(1)}) fusion(f32[4,8,256,128]{3,2,1,0:T(8,128)} %all-gather.3.cloned.1.call-done, f32[4,10,258,130]{3,2,1,0:T(8,128)} %select_maximum_fusion.2, f32[4,1,256,128]{3,2,1,0:T(8,128)} %copy-done.16, f32[4,1,256,128]{3,2,1,0:T(8,128)} %copy-done.15, ...), kind=kLoop, calls=%fused_computation.38 | loop fusion | flops 39845888 | bytes 41943040 | tf_op jit(solution)/shard_map/add | solution.py:101
  147.1 8.5 %fusion.41 = f32[8,256,128,4]{2,3,1,0:T(4,128)S(1)} fusion(f32[4,4,1,1]{1,0,3,2:T(4,128)S(1)} %copy-done.20, f32[4,8,256,128]{3,2,1,0:T(8,128)S(1)} %get-tuple-element.12), kind=kOutput, calls=%fused_computation.69 | convolution fusion | flops 50331648 | bytes 8388672 | tf_op jit(solution)/shard_map/ij,jabc->iabc/dot_general | solution.py:128
  155.6 0.0 copy-start.6
  155.6 0.0 copy-start.12
  155.6 8.7 %fusion.44 = f32[8,256,128,4]{2,3,1,0:T(4,128)S(1)} fusion(f32[4,4,1,1]{1,0,3,2:T(4,128)S(1)} %copy-done.20, f32[4,8,256,128]{3,2,1,0:T(8,128)S(1)} %get-tuple-element.11), kind=kOutput, calls=%fused_computation.73 | convolution fusion | flops 50331648 | bytes 8388672 | tf_op jit(solution)/shard_map/ij,jabc->iabc/dot_general | solution.py:127
  164.4 3.3 %fusion.35 = (f32[4,8,256,128]{3,2,1,0:T(8,128)}, f32[4,8,256,128]{3,2,1,0:T(8,128)S(1)}) fusion(f32[8,256,128,4]{2,3,1,0:T(4,128)S(1)} %fusion.41, f32[8,256,128]{2,1,0:T(8,128)S(1)} %copy-done.6, f32[8,256,128,4]{2,3,1,0:T(4,128)S(1)} %fusion.44, f32[8,256,128]{2,1,0:T(8,128)S(1)} %copy-done.12), kind=kLoop, calls=%fused_computation.62 | loop fusion | flops 13631488 | bytes 18874368 | tf_op jit(solution)/shard_map/mul | solution.py:105
  167.7 2.0 copy-done.2
  169.7 0.1 fusion.61
  169.8 1.3 collective-permute-start.4
  171.1 3.1 %collective-permute-start.5 = (f32[4,1,256,128]{3,2,1,0:T(8,128)S(1)}, f32[4,1,256,128]{3,2,1,0:T(8,128)S(1)}, u32[]{:S(2)}, u32[]{:S(2)}) collective-permute-start(f32[4,1,256,128]{3,2,1,0:T(8,128)S(1)} %get-tuple-element.13), channel_id=1, source_target_pairs={{0,1},{1,2},{2,3},{3,4},{4,5},{5,6},{6,7},{7,8},{8,9},{9,10},{10,1... | collective-permute-start | bytes 1572872 | tf_op jit(solution)/shard_map/ppermute | solution.py:25
  174.1 13.5 %fusion.37 = f32[8,256,128,4]{2,3,1,0:T(4,128)} fusion(f32[4,4,1,1]{1,0,3,2:T(4,128)S(1)} %copy-done.20, f32[4,8,256,128]{3,2,1,0:T(8,128)} %get-tuple-element.6), kind=kOutput, calls=%fused_computation.64 | convolution fusion | flops 50331648 | bytes 8388672 | tf_op jit(solution)/shard_map/ij,jabc->iabc/dot_general | solution.py:128
  187.7 0.0 collective-permute-done.4
  187.7 0.0 collective-permute-done.5
  187.7 0.8 copy-done.14
  188.5 4.5 %select_maximum_fusion = f32[4,10,258,130]{3,2,1,0:T(8,128)S(1)} fusion(f32[4,1,256,128]{3,2,1,0:T(8,128)S(1)} %collective-permute-done.4, f32[4,8,256,128]{3,2,1,0:T(8,128)S(1)} %copy-done.3, f32[4,1,256,128]{3,2,1,0:T(8,128)S(1)} %collective-permute-done.5), kind=kLoop, calls=%fused_computation.4 | loop fusion | flops 20124000 | bytes 10609280 | tf_op jit(solution)/shard_map/concatenate | solution.py:29
  193.1 7.8 %fusion.5 = f32[4,8,256,128]{3,2,1,0:T(8,128)S(1)} fusion(f32[4,8,256,128]{3,2,1,0:T(8,128)S(1)} %copy-done.3, f32[4,10,258,130]{3,2,1,0:T(8,128)S(1)} %select_maximum_fusion, f32[4,1,256,128]{3,2,1,0:T(8,128)} %copy-done.14, f32[4,1,256,128]{3,2,1,0:T(8,128)S(1)} %collective-permute-done.4, f32[8,256,128,4]{2,3,1,0:T(4,128)S(1)} %copy-done.1, ...), kind=kLoop, calls=%fused_computation.18 | loop fusion | flops 30408704 | bytes 38797312 | tf_op jit(solution)/shard_map/add | solution.py:101
  200.8 8.7 %fusion.39 = f32[8,256,128,4]{2,3,1,0:T(4,128)S(1)} fusion(f32[4,4,1,1]{1,0,3,2:T(4,128)S(1)} %copy-done.20, f32[4,8,256,128]{3,2,1,0:T(8,128)S(1)} %fusion.5), kind=kOutput, calls=%fused_computation.66 | convolution fusion | flops 50331648 | bytes 8388672 | tf_op jit(solution)/shard_map/ij,jabc->iabc/dot_general | solution.py:127
  209.6 0.0 copy-start.7
  209.6 2.2 constant_dynamic-slice_fusion
  211.8 0.0 copy-start.13
  211.8 1.6 fusion.46
  213.4 1.6 fusion.47
  (32 shorter events, 0.1 us)
Async XLA Ops:
  7.2 1.5 copy-start.17
  7.2 61.8 %all-gather.3.cloned.1.call-start = ((), (), s32[]{:S(2)}) async-start(), calls=%async_computation | async-start | bytes 6291456 | tf_op jit(solution)/shard_map/all_gather | solution.py:118
  7.9 119.4 %all-gather.5.cloned.1.call-start = ((), (), s32[]{:S(2)}) async-start(), calls=%async_computation.1 | async-start | bytes 6291456 | tf_op jit(solution)/shard_map/all_gather | solution.py:119
  9.0 6.6 %copy-start.11 = (pred[8,256,128]{2,1,0:T(8,128)(4,1)}, pred[8,256,128]{2,1,0:T(8,128)(4,1)S(1)}, u32[]{:S(2)}) copy-start(pred[8,256,128]{2,1,0:T(8,128)(4,1)S(1)} %get-tuple-element.10) | copy-start | bytes 786436
  9.3 4.4 %collective-permute-start = (f32[2,1,256,128]{3,2,1,0:T(8,128)S(1)}, f32[2,1,256,128]{3,2,1,0:T(8,128)S(1)}, u32[]{:S(2)}, u32[]{:S(2)}) collective-permute-start(f32[2,1,256,128]{3,2,1,0:T(8,128)S(1)} %get-tuple-element.20), channel_id=1, source_target_pairs={{1,0},{2,1},{3,2},{4,3},{5,4},{6,5},{7,6},{8,7},{9,8},{10,9},{11,1... | collective-permute-start | bytes 786440 | tf_op jit(solution)/shard_map/ppermute | solution.py:28
  10.6 4.2 %collective-permute-start.2 = (f32[2,1,256,128]{3,2,1,0:T(8,128)S(1)}, f32[2,1,256,128]{3,2,1,0:T(8,128)S(1)}, u32[]{:S(2)}, u32[]{:S(2)}) collective-permute-start(f32[2,1,256,128]{3,2,1,0:T(8,128)S(1)} %get-tuple-element.19), channel_id=1, source_target_pairs={{0,1},{1,2},{2,3},{3,4},{4,5},{5,6},{6,7},{7,8},{8,9},{9,10},{10,1... | collective-permute-start | bytes 786440 | tf_op jit(solution)/shard_map/ppermute | solution.py:25
  13.6 1.1 copy-start.18
  14.8 0.7 copy-start.19
  19.1 108.2 %copy-start.8 = (f32[8,256,128]{2,1,0:T(8,128)}, f32[8,256,128]{2,1,0:T(8,128)S(1)}, u32[]{:S(2)}) copy-start(f32[8,256,128]{2,1,0:T(8,128)S(1)} %get-tuple-element.21) | copy-start | bytes 3145732
  69.0 10.7 %copy-start.4 = (f32[4,8,256,128]{3,2,1,0:T(8,128)S(1)}, f32[4,8,256,128]{3,2,1,0:T(8,128)}, u32[]{:S(2)}) copy-start(f32[4,8,256,128]{3,2,1,0:T(8,128)} %all-gather.3.cloned.1.call-done) | copy-start | bytes 12582916
  70.4 7.5 %collective-permute-start.1 = (f32[4,1,256,128]{3,2,1,0:T(8,128)S(1)}, f32[4,1,256,128]{3,2,1,0:T(8,128)S(1)}, u32[]{:S(2)}, u32[]{:S(2)}) collective-permute-start(f32[4,1,256,128]{3,2,1,0:T(8,128)S(1)} %get-tuple-element.16), channel_id=1, source_target_pairs={{1,0},{2,1},{3,2},{4,3},{5,4},{6,5},{7,6},{8,7},{9,8},{10,9},{11,1... | collective-permute-start | bytes 1572872 | tf_op jit(solution)/shard_map/ppermute | solution.py:28
  71.9 6.1 %collective-permute-start.3 = (f32[4,1,256,128]{3,2,1,0:T(8,128)S(1)}, f32[4,1,256,128]{3,2,1,0:T(8,128)S(1)}, u32[]{:S(2)}, u32[]{:S(2)}) collective-permute-start(f32[4,1,256,128]{3,2,1,0:T(8,128)S(1)} %get-tuple-element.15), channel_id=1, source_target_pairs={{0,1},{1,2},{2,3},{3,4},{4,5},{5,6},{6,7},{7,8},{8,9},{9,10},{10,1... | collective-permute-start | bytes 1572872 | tf_op jit(solution)/shard_map/ppermute | solution.py:25
  77.9 49.4 %copy-start.9 = (f32[8,256,128]{2,1,0:T(8,128)S(1)}, f32[8,256,128]{2,1,0:T(8,128)}, u32[]{:S(2)}) copy-start(f32[8,256,128]{2,1,0:T(8,128)} %get-tuple-element.22) | copy-start | bytes 3145732
  77.9 49.4 %copy-start.10 = (f32[8,256,128]{2,1,0:T(8,128)S(1)}, f32[8,256,128]{2,1,0:T(8,128)}, u32[]{:S(2)}) copy-start(f32[8,256,128]{2,1,0:T(8,128)} %get-tuple-element.23) | copy-start | bytes 3145732
  78.0 0.9 copy-start.15
  78.8 0.9 copy-start.16
  127.3 19.8 %copy-start.20 = (f32[4,4,1,1]{1,0,3,2:T(4,128)S(1)}, f32[4,4,1,1]{1,0,3,2:T(4,128)}, u32[]{:S(2)}) copy-start(f32[4,4,1,1]{1,0,3,2:T(4,128)} %constant.61) | copy-start | bytes 196
  155.6 8.7 %copy-start = (f32[8,256,128,4]{2,3,1,0:T(4,128)}, f32[8,256,128,4]{2,3,1,0:T(4,128)S(1)}, u32[]{:S(2)}) copy-start(f32[8,256,128,4]{2,3,1,0:T(4,128)S(1)} %fusion.41) | copy-start | bytes 12582916
  155.6 8.7 %copy-start.6 = (f32[8,256,128]{2,1,0:T(8,128)S(1)}, f32[8,256,128]{2,1,0:T(8,128)}, u32[]{:S(2)}) copy-start(f32[8,256,128]{2,1,0:T(8,128)} %param.7) | copy-start | bytes 3145732
  155.6 8.7 %copy-start.12 = (f32[8,256,128]{2,1,0:T(8,128)S(1)}, f32[8,256,128]{2,1,0:T(8,128)}, u32[]{:S(2)}) copy-start(f32[8,256,128]{2,1,0:T(8,128)} %param.6) | copy-start | bytes 3145732
  167.7 2.0 copy-start.2
  169.8 17.9 %collective-permute-start.4 = (f32[4,1,256,128]{3,2,1,0:T(8,128)S(1)}, f32[4,1,256,128]{3,2,1,0:T(8,128)S(1)}, u32[]{:S(2)}, u32[]{:S(2)}) collective-permute-start(f32[4,1,256,128]{3,2,1,0:T(8,128)S(1)} %get-tuple-element.14), channel_id=1, source_target_pairs={{1,0},{2,1},{3,2},{4,3},{5,4},{6,5},{7,6},{8,7},{9,8},{10,9},{11,1... | collective-permute-start | bytes 1572872 | tf_op jit(solution)/shard_map/ppermute | solution.py:28
  171.1 16.6 %collective-permute-start.5 = (f32[4,1,256,128]{3,2,1,0:T(8,128)S(1)}, f32[4,1,256,128]{3,2,1,0:T(8,128)S(1)}, u32[]{:S(2)}, u32[]{:S(2)}) collective-permute-start(f32[4,1,256,128]{3,2,1,0:T(8,128)S(1)} %get-tuple-element.13), channel_id=1, source_target_pairs={{0,1},{1,2},{2,3},{3,4},{4,5},{5,6},{6,7},{7,8},{8,9},{9,10},{10,1... | collective-permute-start | bytes 1572872 | tf_op jit(solution)/shard_map/ppermute | solution.py:25
  174.1 14.4 %copy-start.3 = (f32[4,8,256,128]{3,2,1,0:T(8,128)S(1)}, f32[4,8,256,128]{3,2,1,0:T(8,128)}, u32[]{:S(2)}) copy-start(f32[4,8,256,128]{3,2,1,0:T(8,128)} %copy-done.2) | copy-start | bytes 12582916
  187.7 5.4 %copy-start.1 = (f32[8,256,128,4]{2,3,1,0:T(4,128)S(1)}, f32[8,256,128,4]{2,3,1,0:T(4,128)}, u32[]{:S(2)}) copy-start(f32[8,256,128,4]{2,3,1,0:T(4,128)} %copy-done) | copy-start | bytes 12582916
  187.7 0.8 copy-start.14
  200.8 8.8 %copy-start.5 = (f32[8,256,128,4]{2,3,1,0:T(4,128)S(1)}, f32[8,256,128,4]{2,3,1,0:T(4,128)}, u32[]{:S(2)}) copy-start(f32[8,256,128,4]{2,3,1,0:T(4,128)} %fusion.37) | copy-start | bytes 12582916
  209.6 2.2 %copy-start.7 = (f32[8,256,128]{2,1,0:T(8,128)S(1)}, f32[8,256,128]{2,1,0:T(8,128)}, u32[]{:S(2)}) copy-start(f32[8,256,128]{2,1,0:T(8,128)} %param.7) | copy-start | bytes 3145732
  211.8 1.6 copy-start.13
Sparse Core Ops, SparseCore 0:
  9.5 59.4 all-gather.2
  70.5 56.7 all-gather.4
where the time goes:
time: 223 us; the launch traced here: 222 us
  waiting for transfers between devices  93.5 us (42%)
  other arithmetic  52.1 us (23%)
  matrix products  39.5 us (18%)
  between operations  14.4 us (6%)
  starting transfers between devices  13.3 us (6%)
  local copies, waits for them, and re-layouts  9.01 us (4%)
    all_gather x1, waiting for transfers between devices, on_device(): lax.all_gather(u_guess, 'node', axis=0, tiled=True)  49.9 us
    all_gather x1, waiting for transfers between devices, on_device(): lax.all_gather(v_guess, 'node', axis=0, tiled=True)  41.1 us
    add x2, other arithmetic, rates(): rate_u = spread + excite[None] * ionic  27.5 us
    dot_general x2, matrix products, on_device(): jnp.einsum('ij,jabc->iabc', weights_all, rate_v, precision=lax.Precision....  22.1 us
    dot_general x2, matrix products, on_device(): jnp.einsum('ij,jabc->iabc', weights_all, rate_u, precision=lax.Precision....  17.4 us
    concatenate x2, other arithmetic, with_halo(): block = jnp.concatenate([low, block, high], axis=dim)  11 us
    ppermute x3, starting transfers between devices, with_halo(): lax.ppermute(lax.slice_in_dim(block, block.shape[dim] - width, None, axis...  9.17 us
    unnamed x42, local copies, waits for them, and re-layouts  5.31 us
  transfers between devices with their start and end apart: 8, of which 3 were waited for; matrix products, arithmetic and copies ran while one was open for 13% of the time, Pallas kernels for 0%

commit v1 on v0

v1 whole, which is shorter than its diff:
```python
import functools

import jax
import jax.numpy as jnp
from jax import lax
from jax.experimental import pallas as pl
from jax.experimental.pallas import tpu as pltpu
from jax.sharding import PartitionSpec as P

SWEEPS = 2


radau_points = (0.08858795951270396, 0.4094668644407347, 0.7876594617608471, 1.0)
time_step = 0.16
onset_level = 0.15
ionic_gain = 8.0
recovery_base = 0.002
recovery_slope = 0.2
recovery_offset = 0.3
conductances = (1.0, 0.35, 0.05)
excitability = (1.0, 0.6, 0.0)


def weight_table():
    table = []
    for target in range(4):
        entries = []
        for column in range(4):
            coeffs = [1.0]
            for other in range(4):
                if other != column:
                    factor = 1.0 / (radau_points[column] - radau_points[other])
                    raised = [0.0] + coeffs
                    lowered = coeffs + [0.0]
                    coeffs = [
                        factor * (raised[place] - radau_points[other] * lowered[place])
                        for place in range(len(raised))
                    ]
            integral = 0.0
            for place in range(len(coeffs)):
                integral = integral + coeffs[place] * radau_points[target] ** (place + 1) / (
                    place + 1
                )
            entries.append(time_step * integral)
        table.append(entries)
    return table


def label_values(labels, values):
    return jnp.where(
        labels == 0,
        jnp.float32(values[0]),
        jnp.where(labels == 1, jnp.float32(values[1]), jnp.float32(values[2])),
    )


MESH = pl.DeviceIdType.MESH
PAD = 8
ROWS = 16
LAST_ROWS = 32


def kernel(
    node_count, space_count, u_start, v_start, labels, u_guess, v_guess, u_out, v_out,
    u_old, u_new, v_now, u_first, v_first, lab, conduct, face_x, face_y, face_z, excite,
    load_sem, side_send, side_recv, guess_send, guess_recv, v_send, v_recv,
):
    own, planes, height, width = u_guess.shape
    total = own * node_count
    me, place = lax.axis_index("node"), lax.axis_index("space")
    peer = 1 - me
    right = lax.rem(place + 1, space_count)
    left = lax.rem(place + space_count - 1, space_count)
    mine, theirs = pl.ds(me * own, own), pl.ds(peer * own, own)
    inner = pl.ds(PAD, height)
    weights = weight_table()
    last = planes - 2
    order = [0, planes - 1] + list(range(1, last))
    last_tiles = height // LAST_ROWS

    barrier = pltpu.get_barrier_semaphore()
    for target in ({"node": peer}, {"space": left}, {"space": right}):
        pl.semaphore_signal(barrier, inc=1, device_id=target, device_id_type=MESH)

    loads = [
        pltpu.make_async_copy(source, target, load_sem.at[index])
        for index, (source, target) in enumerate((
            (labels, lab.at[pl.ds(1, planes)]),
            (u_guess, u_old.at[mine, pl.ds(1, planes), inner]),
            (v_guess, v_now.at[mine]),
            (u_start, u_first),
            (v_start, v_first),
        ))
    ]
    for load in loads:
        load.start()
    pl.semaphore_wait(barrier, 3)

    def remote(source, target, send, recv, device):
        return pltpu.make_async_remote_copy(
            src_ref=source, dst_ref=target, send_sem=send, recv_sem=recv,
            device_id=device, device_id_type=MESH,
        )

    def side(index, source, target, device):
        return remote(source, target, side_send.at[index], side_recv.at[index], {"space": device})

    def guess(index, first, count):
        return remote(
            u_guess.at[:, pl.ds(first, count)],
            u_old.at[mine, pl.ds(first + 1, count), inner],
            guess_send.at[index], guess_recv.at[index], {"node": peer},
        )

    def recovery_plane(index, plane):
        return remote(
            v_guess.at[:, plane], v_now.at[mine, plane],
            v_send.at[index], v_recv.at[index], {"node": peer},
        )

    def recovery_tile(tile):
        rows = pl.ds(pl.multiple_of(tile * LAST_ROWS, LAST_ROWS), LAST_ROWS)
        index = len(order) + tile
        return remote(
            v_guess.at[:, last, rows], v_now.at[mine, last, rows],
            v_send.at[index], v_recv.at[index], {"node": peer},
        )

    guesses = [guess(0, 0, 1), guess(1, planes - 1, 1), guess(2, 1, planes - 2)]
    recoveries = [recovery_plane(index, plane) for index, plane in enumerate(order)]
    label_sides = [
        side(0, labels.at[planes - 1], lab.at[0], right),
        side(1, labels.at[0], lab.at[planes + 1], left),
    ]
    own_sides = [
        side(2, u_guess.at[:, planes - 1], u_old.at[mine, 0, inner], right),
        side(3, u_guess.at[:, 0], u_old.at[mine, planes + 1, inner], left),
    ]
    for copy in guesses + label_sides + own_sides + recoveries:
        copy.start()

    @pl.loop(0, last_tiles)
    def _(tile):
        recovery_tile(tile).start()

    edge = jnp.zeros((PAD, width), jnp.float32)
    for field in (u_old, u_new):
        for node in range(total):
            for plane in range(1, planes + 1):
                field[node, plane, 0:PAD] = edge
                field[node, plane, PAD + height : PAD + height + PAD] = edge
    for plane in range(planes):
        face_y[plane, 0:PAD] = edge
        conduct[plane + 1, 0:PAD] = edge
        conduct[plane + 1, PAD + height : PAD + height + PAD] = edge

    loads[0].wait()
    for copy in label_sides:
        copy.wait()

    @pl.loop(0, planes + 2)
    def _(plane):
        outside = ((plane == 0) & (place == 0)) | (
            (plane == planes + 1) & (place == space_count - 1)
        )
        scale = jnp.where(outside, jnp.float32(0), jnp.float32(1))

        @pl.loop(0, height // ROWS)
        def _(step):
            row = pl.multiple_of(step * ROWS, ROWS)
            found = label_values(lab[plane, pl.ds(row, ROWS)], conductances)
            conduct[plane, pl.ds(row + PAD, ROWS)] = found * scale

    def face(one, other):
        return 2.0 * one * other / (one + other)

    @pl.loop(0, planes + 1)
    def _(plane):
        @pl.loop(0, height // ROWS)
        def _(step):
            row = pl.multiple_of(step * ROWS, ROWS)
            here = conduct[plane, pl.ds(row + PAD, ROWS)]
            face_x[plane, pl.ds(row, ROWS)] = face(here, conduct[plane + 1, pl.ds(row + PAD, ROWS)])

    @pl.loop(0, planes)
    def _(plane):
        @pl.loop(0, height // ROWS)
        def _(step):
            row = pl.multiple_of(step * ROWS, ROWS)
            here = conduct[plane + 1, pl.ds(row + PAD, ROWS)]
            face_y[plane, pl.ds(row + PAD, ROWS)] = face(
                here, conduct[plane + 1, pl.ds(row + PAD + 1, ROWS)]
            )
            beside = face(here, pltpu.roll(here, width - 1, 1))
            lane = lax.broadcasted_iota(jnp.int32, (ROWS, width), 1)
            face_z[plane, pl.ds(row, ROWS)] = jnp.where(lane == width - 1, 0.0, beside)
            excite[plane, pl.ds(row, ROWS)] = label_values(
                lab[plane + 1, pl.ds(row, ROWS)], excitability
            )

    loads[1].wait()
    guesses[0].wait_recv()
    relays = [side(4, u_old.at[theirs, 1, inner], u_old.at[theirs, planes + 1, inner], left)]
    relays[0].start()
    guesses[1].wait_recv()
    relays.append(side(5, u_old.at[theirs, planes, inner], u_old.at[theirs, 0, inner], right))
    relays[1].start()
    for load in loads[2:]:
        load.wait()
    for copy in own_sides + relays:
        copy.wait()
    guesses[2].wait_recv()

    def sweep(field, plane, first_row, count, table, write):
        @pl.loop(0, count // ROWS)
        def _(step):
            row = pl.multiple_of(first_row + step * ROWS, ROWS)
            rows = pl.ds(row, ROWS)
            mid = pl.ds(row + PAD, ROWS)
            up, down = pl.ds(row + PAD + 1, ROWS), pl.ds(row + PAD - 1, ROWS)
            x_high, x_low = face_x[plane + 1, rows], face_x[plane, rows]
            y_high, y_low = face_y[plane, mid], face_y[plane, down]
            z_high = face_z[plane, rows]
            active = excite[plane, rows]
            sums_u = [u_first[plane, rows]] * len(table)
            sums_v = [v_first[plane, rows]] * len(table)
            for node in range(total):
                u = field[node, plane + 1, mid]
                v = v_now[node, plane, rows]
                flux = z_high * (pltpu.roll(u, width - 1, 1) - u)
                spread = flux - pltpu.roll(flux, 1, 1)
                spread += x_high * (field[node, plane + 2, mid] - u)
                spread += x_low * (field[node, plane, mid] - u)
                spread += y_high * (field[node, plane + 1, up] - u)
                spread += y_low * (field[node, plane + 1, down] - u)
                gained = ionic_gain * u
                ionic = gained * (u - onset_level) * (1.0 - u) - u * v
                rate_u = spread + active * ionic
                recovery = recovery_base + recovery_slope * v / jnp.maximum(
                    u + recovery_offset, recovery_offset
                )
                rate_v = recovery * (-v - gained * (u - onset_level - 1.0))
                for target in range(len(table)):
                    sums_u[target] = sums_u[target] + table[target][node] * rate_u
                    sums_v[target] = sums_v[target] + table[target][node] * rate_v
            for target in range(len(table)):
                write(target, plane, row, sums_u[target], sums_v[target])

    def write_first(target, plane, row, u, v):
        u_new[target, plane + 1, pl.ds(row + PAD, ROWS)] = u
        v_now[target, plane, pl.ds(row, ROWS)] = v

    def write_second(target, plane, row, u, v):
        u_out[target, plane, pl.ds(row, ROWS)] = u
        v_out[target, plane, pl.ds(row, ROWS)] = v

    table_first = [[jnp.float32(value) for value in line] for line in weights]
    table_second = []
    for target in range(own):
        line = []
        for node in range(total):
            value = jnp.float32(weights[target][node])
            for rank in range(1, node_count):
                value = jnp.where(me == rank, jnp.float32(weights[rank * own + target][node]), value)
            line.append(value)
        table_second.append(line)

    def first(plane, row=0, count=height):
        sweep(u_old, plane, row, count, table_first, write_first)

    def second(plane, row=0, count=height):
        sweep(u_new, plane, row, count, table_second, write_second)

    new_sides = [
        side(6, u_new.at[:, 1, inner], u_new.at[:, planes + 1, inner], left),
        side(7, u_new.at[:, planes, inner], u_new.at[:, 0, inner], right),
    ]
    for index, plane in enumerate(order):
        recoveries[index].wait_recv()
        first(plane)
        if plane == 1:
            for copy in new_sides:
                copy.start()
        if 2 <= plane < planes - 1:
            second(plane - 1)
        if plane == planes - 4:
            new_sides[0].wait_recv()
            new_sides[1].wait_recv()
            second(0)

    @pl.loop(0, last_tiles)
    def _(tile):
        recovery_tile(tile).wait_recv()
        row = pl.multiple_of(tile * LAST_ROWS, LAST_ROWS)
        first(last, row, LAST_ROWS)
        second(last - 1, row, LAST_ROWS)
        second(planes - 1, row, LAST_ROWS)

        @pl.when(tile > 0)
        def _():
            second(last, pl.multiple_of(row - LAST_ROWS, LAST_ROWS), LAST_ROWS)

    second(last, height - LAST_ROWS, LAST_ROWS)

    for copy in guesses + new_sides + recoveries:
        copy.wait_send()

    @pl.loop(0, last_tiles)
    def _(tile):
        recovery_tile(tile).wait_send()


def on_device(mesh, u_start, v_start, labels, u_guess, v_guess):
    own, planes, height, width = u_guess.shape
    node_count, space_count = mesh.shape["node"], mesh.shape["space"]
    assert node_count == 2
    total = own * node_count
    padded = (planes + 2, height + 2 * PAD, width)
    slab = (planes, height, width)
    copies = planes - 1 + height // LAST_ROWS
    result = jax.ShapeDtypeStruct(u_guess.shape, jnp.float32)
    dma = pltpu.SemaphoreType.DMA
    f32 = jnp.float32
    return pl.pallas_call(
        functools.partial(kernel, node_count, space_count),
        out_shape=(result, result),
        in_specs=[pl.BlockSpec(memory_space=pl.ANY)] * 5,
        out_specs=(pl.BlockSpec(memory_space=pltpu.VMEM),) * 2,
        scratch_shapes=[
            pltpu.VMEM((total,) + padded, f32),
            pltpu.VMEM((total,) + padded, f32),
            pltpu.VMEM((total,) + slab, f32),
            pltpu.VMEM(slab, f32),
            pltpu.VMEM(slab, f32),
            pltpu.VMEM((planes + 2, height, width), jnp.int32),
            pltpu.VMEM(padded, f32),
            pltpu.VMEM((planes + 1, height, width), f32),
            pltpu.VMEM((planes, height + 2 * PAD, width), f32),
            pltpu.VMEM(slab, f32),
            pltpu.VMEM(slab, f32),
            dma((5,)), dma((8,)), dma((8,)), dma((3,)), dma((3,)), dma((copies,)), dma((copies,)),
        ],
        compiler_params=pltpu.CompilerParams(collective_id=0, has_side_effects=True),
    )(u_start, v_start, labels, u_guess, v_guess)


def solution(mesh):
    return jax.shard_map(
        functools.partial(on_device, mesh),
        mesh=mesh,
        in_specs=(
            P("space", None, None),
            P("space", None, None),
            P("space", None, None),
            P("node", "space", None, None),
            P("node", "space", None, None),
        ),
        out_specs=(P("node", "space", None, None), P("node", "space", None, None)),
        check_vma=False,
    )
```

time: 223 us -> 118 us (0.53)
  Pallas kernels: 0 us -> 113 us
  waiting for transfers between devices: 93.5 us -> 0 us
  other arithmetic: 52.1 us -> 0 us
  matrix products: 39.5 us -> 0 us
  between operations: 14.4 us -> 0.65 us
  starting transfers between devices: 13.3 us -> 0 us
  local copies, waits for them, and re-layouts: 9.01 us -> 4.58 us
    pallas_call x0 -> x1, Pallas kernels: none -> 113 us  [on_device(): pl.pallas_call(functools.partial(kernel, node_count, space_count), out_sh...]
    all_gather x2 -> x0, waiting for transfers between devices: 91 us -> none  [the longest x1 49.9 us: on_device(): lax.all_gather(u_guess, 'node', axis=0, tiled=True)]
    dot_general x4 -> x0, matrix products: 39.5 us -> none  [the longest x2 22.1 us: on_device(): jnp.einsum('ij,jabc->iabc', weights_all, rate_v, precision=lax.Precision....]
    add x2 -> x0, other arithmetic: 27.5 us -> none  [rates(): rate_u = spread + excite[None] * ionic]
    ppermute x6 -> x0, starting transfers between devices: 13.2 us -> none  [the longest x3 9.17 us: with_halo(): lax.ppermute(lax.slice_in_dim(block, block.shape[dim] - width, None, axis...]
    concatenate x2 -> x0, other arithmetic: 11 us -> none  [with_halo(): block = jnp.concatenate([low, block, high], axis=dim)]
    mul x2 -> x0, other arithmetic: 6.29 us -> none  [the longest x1 3.29 us: rates(): recovery * (-v_field - ionic_gain * u_field * (u_field - onset_level - 1.0))]
    select_n x1 -> x0, other arithmetic: 3.48 us -> none  [face_terms(): jnp.where(total > 0, 2.0 * center * beside / jnp.where(total > 0, total,...]
  transfers between devices with their start and end apart: 8 -> 0, of which waited for: 3 -> 0; matrix products, arithmetic and copies ran while one was open for 13% -> 0% of each run, Pallas kernels for 0% -> 0%
where the time goes in v1:
time: 118 us
  Pallas kernels  113 us (96%)
  local copies, waits for them, and re-layouts  4.58 us (4%)
    pallas_call x1, Pallas kernels, on_device(): pl.pallas_call(functools.partial(kernel, node_count, space_count), out_sh...  113 us
    unnamed x4, local copies, waits for them, and re-layouts  4.58 us

profile of v1, /device:TPU:0, one launch (start us, length us, event | category | flops | bytes accessed | tf_op | source)
XLA Modules:
  0.0 118.1 jit_solution(9252699177804979657)
XLA Ops:
  0.6 112.9 %shard_map.68 = (f32[2,8,256,128]{3,2,1,0:T(8,128)}, f32[2,8,256,128]{3,2,1,0:T(8,128)}) custom-call(f32[8,256,128]{2,1,0:T(8,128)} %u_start.1, f32[8,256,128]{2,1,0:T(8,128)} %v_start.1, s32[8,256,128]{2,1,0:T(8,128)} %labels.1, f32[2,8,256,128]{3,2,1,0:T(8,128)} %u_guess.1, f32[2,8,256,128]{3,2,1,0:T(8,128)} %v_guess.1), custom_call_target="tpu_custom_call" | custom-call | tf_op jit(solution)/shard_map/pallas_call | solution.py:324
  113.5 0.0 copy-start
  113.5 3.3 %copy.9 = f32[2,8,256,128]{3,2,1,0:T(8,128)} copy(f32[2,8,256,128]{3,2,1,0:T(8,128)} %get-tuple-element.4) | data formatting | bytes 4194304
  116.8 0.0 copy-done
  116.8 1.3 %copy.10 = f32[2,8,256,128]{3,2,1,0:T(8,128)} copy(f32[2,8,256,128]{3,2,1,0:T(8,128)S(1)} %copy-done) | data formatting | bytes 4194304
Async XLA Ops:
  113.5 3.3 %copy-start = (f32[2,8,256,128]{3,2,1,0:T(8,128)S(1)}, f32[2,8,256,128]{3,2,1,0:T(8,128)}, u32[]{:S(2)}) copy-start(f32[2,8,256,128]{3,2,1,0:T(8,128)} %get-tuple-element.5) | copy-start | bytes 6291460

commit v2 on v1

--- a/solution.py
+++ b/solution.py
@@ -57,7 +57,10 @@
 MESH = pl.DeviceIdType.MESH
 PAD = 8
 ROWS = 16
-LAST_ROWS = 32
+VMEM_LIMIT = 46 * 2**20
+LAST_ROWS = 64
+WINDOW = 5
+TILE_WINDOW = 4
 
 
 def kernel(
@@ -136,12 +139,16 @@
         side(2, u_guess.at[:, planes - 1], u_old.at[mine, 0, inner], right),
         side(3, u_guess.at[:, 0], u_old.at[mine, planes + 1, inner], left),
     ]
-    for copy in guesses + label_sides + own_sides + recoveries:
+    queue = guesses + recoveries + [recovery_tile(tile) for tile in range(TILE_WINDOW)]
+
+    def advance(count=1):
+        for copy in queue[:count]:
+            copy.start()
+        del queue[:count]
+
+    advance(WINDOW)
+    for copy in label_sides + own_sides:
         copy.start()
-
-    @pl.loop(0, last_tiles)
-    def _(tile):
-        recovery_tile(tile).start()
 
     edge = jnp.zeros((PAD, width), jnp.float32)
     for field in (u_old, u_new):
@@ -210,6 +217,7 @@
     for copy in own_sides + relays:
         copy.wait()
     guesses[2].wait_recv()
+    advance()
 
     def sweep(field, plane, first_row, count, table, write):
         @pl.loop(0, count // ROWS)
@@ -277,6 +285,7 @@
     ]
     for index, plane in enumerate(order):
         recoveries[index].wait_recv()
+        advance(1 if index + 1 < len(order) else len(queue))
         first(plane)
         if plane == 1:
             for copy in new_sides:
@@ -291,6 +300,11 @@
     @pl.loop(0, last_tiles)
     def _(tile):
         recovery_tile(tile).wait_recv()
+
+        @pl.when(tile + TILE_WINDOW < last_tiles)
+        def _():
+            recovery_tile(tile + TILE_WINDOW).start()
+
         row = pl.multiple_of(tile * LAST_ROWS, LAST_ROWS)
         first(last, row, LAST_ROWS)
         second(last - 1, row, LAST_ROWS)
@@ -324,7 +338,7 @@
     return pl.pallas_call(
         functools.partial(kernel, node_count, space_count),
         out_shape=(result, result),
-        in_specs=[pl.BlockSpec(memory_space=pl.ANY)] * 5,
+        in_specs=[pl.BlockSpec(memory_space=pltpu.HBM)] * 5,
         out_specs=(pl.BlockSpec(memory_space=pltpu.VMEM),) * 2,
         scratch_shapes=[
             pltpu.VMEM((total,) + padded, f32),
@@ -340,7 +354,9 @@
             pltpu.VMEM(slab, f32),
             dma((5,)), dma((8,)), dma((8,)), dma((3,)), dma((3,)), dma((copies,)), dma((copies,)),
         ],
-        compiler_params=pltpu.CompilerParams(collective_id=0, has_side_effects=True),
+        compiler_params=pltpu.CompilerParams(
+            collective_id=0, has_side_effects=True, vmem_limit_bytes=VMEM_LIMIT
+        ),
     )(u_start, v_start, labels, u_guess, v_guess)
 
 

time: 118 us -> 118 us (level)
  Pallas kernels: 113 us -> 111 us
  local copies, waits for them, and re-layouts: 4.58 us -> 6.31 us
    pallas_call x1, Pallas kernels: 113 us -> 111 us  [on_device(): pl.pallas_call(functools.partial(kernel, node_count, space_count), out_sh...]
    unnamed x4 -> x8, local copies, waits for them, and re-layouts: 4.58 us -> 6.31 us
where the time goes in v2:
time: 118 us
  Pallas kernels  111 us (94%)
  local copies, waits for them, and re-layouts  6.31 us (5%)
    pallas_call x1, Pallas kernels, on_device(): pl.pallas_call(functools.partial(kernel, node_count, space_count), out_sh...  111 us
    unnamed x8, local copies, waits for them, and re-layouts  6.31 us

profile of v2, /device:TPU:0, one launch (start us, length us, event | category | flops | bytes accessed | tf_op | source)
XLA Modules:
  0.0 117.8 jit_solution(1334098441569127298)
XLA Ops:
  0.6 0.0 copy-start
  0.6 1.2 %copy-done = f32[8,256,128]{2,1,0:T(8,128)S(1)} copy-done((f32[8,256,128]{2,1,0:T(8,128)S(1)}, f32[8,256,128]{2,1,0:T(8,128)}, u32[]{:S(2)}) %copy-start) | copy-done | bytes 1048600
  1.9 0.0 copy-start.1
  1.9 1.2 %copy-done.1 = f32[8,256,128]{2,1,0:T(8,128)S(1)} copy-done((f32[8,256,128]{2,1,0:T(8,128)S(1)}, f32[8,256,128]{2,1,0:T(8,128)}, u32[]{:S(2)}) %copy-start.1) | copy-done | bytes 1048600
  3.1 0.0 copy-start.2
  3.1 1.2 %copy-done.2 = s32[8,256,128]{2,1,0:T(8,128)S(1)} copy-done((s32[8,256,128]{2,1,0:T(8,128)S(1)}, s32[8,256,128]{2,1,0:T(8,128)}, u32[]{:S(2)}) %copy-start.2) | copy-done | bytes 1048600
  4.3 110.8 %shard_map.68 = (f32[2,8,256,128]{3,2,1,0:T(8,128)S(1)}, f32[2,8,256,128]{3,2,1,0:T(8,128)S(1)}) custom-call(f32[8,256,128]{2,1,0:T(8,128)S(1)} %copy-done, f32[8,256,128]{2,1,0:T(8,128)S(1)} %copy-done.1, s32[8,256,128]{2,1,0:T(8,128)S(1)} %copy-done.2, f32[2,8,256,128]{3,2,1,0:T(8,128)} %u_guess.1, f32[2,8,256,128]{3,2,1,0:T(8,128)} %v_guess.1), custom_call_target="tpu_custom_call" | custom-call | tf_op jit(solution)/shard_map/pallas_call | solution.py:338
  115.1 1.3 %copy.9 = f32[2,8,256,128]{3,2,1,0:T(8,128)} copy(f32[2,8,256,128]{3,2,1,0:T(8,128)S(1)} %get-tuple-element.4) | data formatting | bytes 4194304
  116.4 1.3 %copy.10 = f32[2,8,256,128]{3,2,1,0:T(8,128)} copy(f32[2,8,256,128]{3,2,1,0:T(8,128)S(1)} %get-tuple-element.5) | data formatting | bytes 4194304
Async XLA Ops:
  0.6 1.2 %copy-start = (f32[8,256,128]{2,1,0:T(8,128)S(1)}, f32[8,256,128]{2,1,0:T(8,128)}, u32[]{:S(2)}) copy-start(f32[8,256,128]{2,1,0:T(8,128)} %u_start.1) | copy-start | bytes 3145732
  1.9 1.2 %copy-start.1 = (f32[8,256,128]{2,1,0:T(8,128)S(1)}, f32[8,256,128]{2,1,0:T(8,128)}, u32[]{:S(2)}) copy-start(f32[8,256,128]{2,1,0:T(8,128)} %v_start.1) | copy-start | bytes 3145732
  3.1 1.2 %copy-start.2 = (s32[8,256,128]{2,1,0:T(8,128)S(1)}, s32[8,256,128]{2,1,0:T(8,128)}, u32[]{:S(2)}) copy-start(s32[8,256,128]{2,1,0:T(8,128)} %labels.1) | copy-start | bytes 3145732
